TPU v7x, 32 devices: a whole 2x2x4 slice. The times are simulated.
32 devices in a mesh: rep: 4 (over z), own: 8 (over y, x, core).
Axes of the slice: x: 2, y: 2, z: 4, core: 2. Of those that a mesh axis runs over, the one named last changes fastest.
Arguments:
- grads: float32 [16, 576, 1024], P('rep', 'own'), may hold values from -60 to 60
- momentum: bfloat16 [32, 576, 1024], P(('rep', 'own')), may hold values from -6 to 6
- owner_table: int32 [4, 8], replicated, may hold values from 0 to 7, each once within a row
Outputs:
- new_momentum: bfloat16 [32, 576, 1024], P(('rep', 'own'))
- updates: bfloat16 [16, 576, 1024], P(None, 'own')
Inputs may be any that keep to these rules, and one draw needn't show every extreme that they name: Each row of owner_table is a permutation of 0 to 7; entries of 4 or more mark empty slots.
All inputs are finite; a program needn't handle non-finite values.
Results may differ from a plain program's by a relative error of at most 0.01.
Values may be sent and summed in bfloat16 or wider, within the bound.
No kernel may reach another device: no remote copies, remote signals or barrier semaphores. Data moves between devices by JAX's collectives and lax.ppermute only.
A program may use at most 128 MiB of HBM per device.

v0:
```python
import math
import jax
import jax.numpy as jnp
from jax import lax
from jax.sharding import PartitionSpec as P

ITERS = 2
DECAY = 0.95
COEF_A = 3.4445
COEF_B = -4.775
COEF_C = 2.0315
EPSILON = 1e-07


def orthogonalize(blend):
    total = jnp.sqrt(jnp.sum(blend * blend))
    iterate = (blend / (total + EPSILON)).astype(jnp.bfloat16)
    factor = 0.2 * math.sqrt(max(blend.shape[0], blend.shape[1]))
    result = None
    for turn in range(ITERS):
        gram = jnp.dot(iterate, iterate.T, preferred_element_type=jnp.float32).astype(jnp.bfloat16)
        square = jnp.dot(gram, gram, preferred_element_type=jnp.float32)
        poly = (COEF_B * gram.astype(jnp.float32) + COEF_C * square).astype(jnp.bfloat16)
        mixed = COEF_A * iterate.astype(jnp.float32) + jnp.dot(
            poly, iterate, preferred_element_type=jnp.float32
        )
        if turn + 1 < ITERS:
            iterate = mixed.astype(jnp.bfloat16)
        else:
            result = (factor * mixed).astype(jnp.bfloat16)
    return result


def body(grads, momentum, owner_table):
    group = lax.axis_index("rep")
    slot_matrix = lax.dynamic_index_in_dim(owner_table, group, 0, keepdims=False)
    matrix_count, shard_rows, columns = grads.shape
    is_live = slot_matrix < matrix_count
    clamped = jnp.minimum(slot_matrix, matrix_count - 1)
    half_grads = grads.astype(jnp.bfloat16)
    outgoing = jnp.take(half_grads, clamped, axis=0) * is_live[:, None, None].astype(jnp.bfloat16)
    incoming = lax.all_to_all(outgoing, "own", split_axis=0, concat_axis=1, tiled=True)
    gradient = incoming[0].astype(jnp.float32)
    moment = DECAY * momentum[0].astype(jnp.float32) + gradient
    new_momentum = moment.astype(jnp.bfloat16)[None]
    update = orthogonalize(gradient + DECAY * moment)
    returned = lax.all_to_all(update[None], "own", split_axis=1, concat_axis=0, tiled=True)
    holders = jnp.argsort(slot_matrix)[:matrix_count]
    grouped = jnp.take(returned, holders, axis=0)
    updates = lax.all_gather(grouped, "rep", axis=0, tiled=True)
    return (new_momentum, updates)


def solution(mesh):
    in_specs = (P("rep", "own", None), P(("rep", "own"), None, None), P())
    out_specs = (P(("rep", "own"), None, None), P(None, "own", None))
    return jax.shard_map(body, mesh=mesh, in_specs=in_specs, out_specs=out_specs, check_vma=False)
```

profile of v0, /device:TPU:0, one launch (start us, length us, event | category | flops | bytes accessed | tf_op | source)
XLA Modules:
  0.0 138.9 jit_solution(14850939103805925869)
XLA Ops:
  7.2 0.7 compare_convert_fusion
  7.9 0.7 fusion.10
  8.6 1.4 convert_element_type.90
  9.9 0.6 gather_fusion
  10.6 0.2 select_multiply_fusion
  10.8 21.7 %all_to_all.21 = bf16[8,72,1024]{2,1,0:T(8,128)(2,1)S(1)} all-to-all(bf16[8,72,1024]{2,1,0:T(8,128)(2,1)S(1)} %select_multiply_fusion), channel_id=1, replica_groups=mesh['rep'=4,'own'=8] {'own'}, dimensions={0} | all-to-all | bytes 2359296 | tf_op jit(solution)/shard_map/all_to_all | solution.py:42
  32.5 0.0 copy-start
  32.5 0.3 convert_element_type.111
  32.8 1.0 copy-done
  33.8 1.5 %convert_multiply_fusion = (f32[1,576,1024]{2,1,0:T(8,128)S(1)}, bf16[1,576,1024]{2,1,0:T(8,128)(2,1)}) fusion(bf16[1,576,1024]{2,1,0:T(8,128)(2,1)S(1)} %copy-done, f32[1,576,1024]{2,1,0:T(8,128)S(1)} %bitcast.46), kind=kLoop, calls=%fused_computation.13 | loop fusion | flops 2359296 | bytes 7077888 | tf_op jit(solution)/shard_map/mul | solution.py:44
  35.3 1.2 multiply_reduce_fusion
  37.2 0.5 divide_convert_fusion
  37.7 0.0 copy-start.1
  37.7 1.1 convolution_convert_fusion.1
  38.8 0.1 copy-done.1
  39.0 0.6 fusion.4
  39.6 1.7 %add_convert_fusion = bf16[576,1024]{1,0:T(8,128)(2,1)S(1)} fusion(bf16[576,1024]{1,0:T(8,128)(2,1)S(1)} %fusion.4, bf16[576,576]{1,0:T(8,128)(2,1)S(1)} %convolution_convert_fusion.1), kind=kOutput, calls=%fused_computation.9 | convolution fusion | flops 1065701376 | bytes 3022848 | tf_op jit(solution)/shard_map/dot_general | solution.py:24
  41.3 1.1 convolution_convert_fusion
  42.4 1.7 %fusion.5 = bf16[1,576,1024]{2,1,0:T(8,128)(2,1)S(1)} fusion(bf16[576,1024]{1,0:T(8,128)(2,1)S(1)} %add_convert_fusion, bf16[576,576]{1,0:T(8,128)(2,1)S(1)} %convolution_convert_fusion), kind=kOutput, calls=%fused_computation.17 | convolution fusion | flops 1066291200 | bytes 3022848 | tf_op jit(solution)/shard_map/dot_general | solution.py:24
  44.1 1.8 %copy.9 = bf16[1,576,1024]{2,0,1:T(2,128)(2,1)S(1)} copy(bf16[1,576,1024]{2,1,0:T(8,128)(2,1)S(1)} %fusion.5) | data formatting | bytes 2359296 | tf_op jit(solution)/shard_map/broadcast_in_dim | solution.py:47
  46.0 0.5 broadcast.140
  46.5 7.7 %reduce.3 = bf16[576,1024]{1,0:T(8,128)(2,1)S(1)} reduce(bf16[576,1,1024]{2,1,0:T(2,128)(2,1)S(1)} %bitcast.47, bf16[]{:T(256)} %broadcast.140), dimensions={1}, to_apply=%bitcast.43.reduce_sub_computation | reduce | bytes 2359298
  54.2 1.6 %reshape.107 = bf16[8,2,36864]{2,1,0:T(2,128)(2,1)} reshape(bf16[576,1024]{1,0:T(8,128)(2,1)S(1)} %reduce.3) | data formatting | bytes 2359296
  55.8 3.6 %all-to-all-start.1 = ((bf16[8,2,36864]{2,1,0:T(2,128)(2,1)}), bf16[8,2,36864]{2,1,0:T(2,128)(2,1)S(1)}, u32[]{:S(2)}, u32[]{:S(2)}) async-start(bf16[8,2,36864]{2,1,0:T(2,128)(2,1)} %reshape.107), calls=%async_computation.1 | async-start | bytes 2359296 | tf_op jit(solution)/shard_map/all_to_all | solution.py:47
  59.4 0.0 all-gather.2.cloned.1.call-start
  59.4 1.0 sort.17
  60.5 15.6 %all-to-all-done.1 = bf16[8,2,36864]{2,1,0:T(2,128)(2,1)S(1)} async-done(((bf16[8,2,36864]{2,1,0:T(2,128)(2,1)}), bf16[8,2,36864]{2,1,0:T(2,128)(2,1)S(1)}, u32[]{:S(2)}, u32[]{:S(2)}) %all-to-all-start.1) | async-done | bytes 1179680 | tf_op jit(solution)/shard_map/all_to_all | solution.py:47
  76.1 1.1 reshape.108
  77.2 0.4 copy.7
  77.7 0.6 gather_fusion.1
  78.3 0.9 broadcast_select_fusion
  79.2 0.0 all-gather.2.cloned.1.call-update
  79.2 49.5 %all-gather.2.cloned.1.call-done = bf16[16,72,1024]{2,1,0:T(8,128)(2,1)} async-done(((bf16[4,72,1024]{2,1,0:T(8,128)(2,1)}), bf16[16,72,1024]{2,1,0:T(8,128)(2,1)}) %all-gather.2.cloned.1.call-update) | async-done | bytes 2359312 | tf_op jit(solution)/shard_map/all_gather | solution.py:50
  128.8 3.3 %copy.11 = bf16[16,72,1024]{2,1,0:T(8,128)(2,1)} copy(bf16[16,72,1024]{2,1,0:T(8,128)(2,1)} %all-gather.2.cloned.1.call-done) | data formatting | bytes 4718592
  (5 shorter events, 0.0 us)
Async XLA Ops:
  32.5 1.3 copy-start
  37.7 1.3 copy-start.1
  55.8 20.3 %all-to-all-start.1 = ((bf16[8,2,36864]{2,1,0:T(2,128)(2,1)}), bf16[8,2,36864]{2,1,0:T(2,128)(2,1)S(1)}, u32[]{:S(2)}, u32[]{:S(2)}) async-start(bf16[8,2,36864]{2,1,0:T(2,128)(2,1)} %reshape.107), calls=%async_computation.1 | async-start | bytes 2359296 | tf_op jit(solution)/shard_map/all_to_all | solution.py:47
  59.4 69.4 %all-gather.2.cloned.1.call-start = ((), (), s32[]{:S(2)}) async-start(), calls=%async_computation.2 | async-start | bytes 2949120 | tf_op jit(solution)/shard_map/all_gather | solution.py:50
Sparse Core Ops, SparseCore 0:
  79.4 49.3 all-gather.1
where the time goes:
time: 139 us
  waiting for transfers between devices  65.1 us (47%)
  blocking collectives  21.7 us (16%)
  other arithmetic  16.7 us (12%)
  between operations  14.9 us (11%)
  local copies, waits for them, and re-layouts  11.1 us (8%)
  matrix products  5.68 us (4%)
  starting transfers between devices  3.61 us (3%)
    all_gather x1, waiting for transfers between devices, body(): updates = lax.all_gather(grouped, 'rep', axis=0, tiled=True)  49.5 us
    all_to_all x1, blocking collectives, body(): lax.all_to_all(outgoing, 'own', split_axis=0, concat_axis=1, tiled=True)  21.7 us
    all_to_all x1, waiting for transfers between devices, body(): lax.all_to_all(update[None], 'own', split_axis=1, concat_axis=0, tiled=True)  15.6 us
    unnamed x9, local copies, waits for them, and re-layouts  8.11 us
    unnamed x1, other arithmetic  7.72 us
    all_to_all x1, starting transfers between devices, body(): lax.all_to_all(update[None], 'own', split_axis=1, concat_axis=0, tiled=True)  3.56 us
    dot_general x2, matrix products, orthogonalize(): jnp.dot(poly, iterate, preferred_element_type=jnp.float32)  3.45 us
  transfers between devices with their start and end apart: 2, of which 2 were waited for; matrix products, arithmetic and copies ran while one was open for 1% of the time, Pallas kernels for 0%

commit v1 on v0

--- a/solution.py
+++ b/solution.py
@@ -44,7 +44,12 @@
     moment = DECAY * momentum[0].astype(jnp.float32) + gradient
     new_momentum = moment.astype(jnp.bfloat16)[None]
     update = orthogonalize(gradient + DECAY * moment)
-    returned = lax.all_to_all(update[None], "own", split_axis=1, concat_axis=0, tiled=True)
+    returned = jnp.concatenate(
+        lax.all_to_all(
+            jnp.stack(jnp.split(update[None], lax.axis_size("own"), axis=1)), "own", 0, 0
+        ),
+        axis=0,
+    )
     holders = jnp.argsort(slot_matrix)[:matrix_count]
     grouped = jnp.take(returned, holders, axis=0)
     updates = lax.all_gather(grouped, "rep", axis=0, tiled=True)

time: 139 us -> 134 us (0.964)
  other arithmetic: 16.7 us -> 9.06 us
  matrix products: 5.68 us -> 8.51 us
    unnamed x1 -> x0, other arithmetic: 7.72 us -> none
    dot_general x2, matrix products: 3.45 us -> 5.42 us  [orthogonalize(): jnp.dot(poly, iterate, preferred_element_type=jnp.float32)]
    broadcast_in_dim x1 -> x0, local copies, waits for them, and re-layouts: 1.82 us -> none  [body(): update[None]]
    unnamed x9 -> x12, local copies, waits for them, and re-layouts: 8.11 us -> 8.99 us
where the time goes in v1:
time: 134 us
  waiting for transfers between devices  65.1 us (49%)
  blocking collectives  21.7 us (16%)
  between operations  14.8 us (11%)
  local copies, waits for them, and re-layouts  10.9 us (8%)
  other arithmetic  9.06 us (7%)
  matrix products  8.51 us (6%)
  starting transfers between devices  3.61 us (3%)
    all_gather x1, waiting for transfers between devices, body(): updates = lax.all_gather(grouped, 'rep', axis=0, tiled=True)  49.5 us
    all_to_all x1, blocking collectives, body(): lax.all_to_all(outgoing, 'own', split_axis=0, concat_axis=1, tiled=True)  21.7 us
    all_to_all x1, waiting for transfers between devices, body(): lax.all_to_all(jnp.stack(jnp.split(update[None], lax.axis_size('own'), ax...  15.6 us
    unnamed x12, local copies, waits for them, and re-layouts  8.99 us
    dot_general x2, matrix products, orthogonalize(): jnp.dot(poly, iterate, preferred_element_type=jnp.float32)  5.42 us
    all_to_all x1, starting transfers between devices, body(): lax.all_to_all(jnp.stack(jnp.split(update[None], lax.axis_size('own'), ax...  3.56 us
    dot_general x2, matrix products, orthogonalize(): jnp.dot(iterate, iterate.T, preferred_element_type=jnp.float32)  3.1 us
  transfers between devices with their start and end apart: 2, of which 2 were waited for; matrix products, arithmetic and copies ran while one was open for 1% of the time, Pallas kernels for 0%

profile of v1, /device:TPU:0, one launch (start us, length us, event | category | flops | bytes accessed | tf_op | source)
XLA Modules:
  0.0 133.8 jit_solution(13756480437863896277)
XLA Ops:
  7.2 0.7 compare_convert_fusion
  7.9 0.7 fusion.18
  8.6 1.4 %convert_element_type.90 = bf16[4,72,1024]{2,1,0:T(8,128)(2,1)S(1)} convert(f32[4,72,1024]{2,1,0:T(8,128)} %param.3) | non-fusion elementwise | flops 294912 | bytes 1769472 | tf_op jit(solution)/shard_map/convert_element_type | solution.py:40
  9.9 0.6 gather_fusion
  10.6 0.2 select_multiply_fusion
  10.7 21.7 %all_to_all.14 = bf16[8,72,1024]{2,1,0:T(8,128)(2,1)S(1)} all-to-all(bf16[8,72,1024]{2,1,0:T(8,128)(2,1)S(1)} %select_multiply_fusion), channel_id=1, replica_groups=mesh['rep'=4,'own'=8] {'own'}, dimensions={0} | all-to-all | bytes 2359296 | tf_op jit(solution)/shard_map/all_to_all | solution.py:42
  32.5 0.0 copy-start
  32.5 0.3 convert_element_type.111
  32.8 1.0 copy-done
  33.7 1.5 %convert_multiply_fusion = (f32[1,576,1024]{2,1,0:T(8,128)S(1)}, bf16[1,576,1024]{2,1,0:T(8,128)(2,1)}) fusion(bf16[1,576,1024]{2,1,0:T(8,128)(2,1)S(1)} %copy-done, f32[1,576,1024]{2,1,0:T(8,128)S(1)} %bitcast.74), kind=kLoop, calls=%fused_computation.13 | loop fusion | flops 2359296 | bytes 7077888 | tf_op jit(solution)/shard_map/mul | solution.py:44
  35.3 1.3 multiply_reduce_fusion
  37.2 0.5 divide_convert_fusion
  37.7 0.0 copy-start.1
  37.7 2.0 %convolution_convert_fusion.1 = bf16[576,576]{1,0:T(8,128)(2,1)} fusion(bf16[576,1024]{1,0:T(8,128)(2,1)S(1)} %bitcast.76), kind=kOutput, calls=%fused_computation.19 | convolution fusion | flops 679809024 | bytes 1843200 | tf_op jit(solution)/shard_map/dot_general | solution.py:21
  39.7 0.0 copy-done.1
  39.7 0.6 fusion.4
  40.3 3.6 %add_convert_fusion = bf16[576,1024]{1,0:T(8,128)(2,1)S(1)} fusion(bf16[576,1024]{1,0:T(8,128)(2,1)S(1)} %fusion.4, bf16[576,576]{1,0:T(8,128)(2,1)} %convolution_convert_fusion.1), kind=kOutput, calls=%fused_computation.9 | convolution fusion | flops 1065701376 | bytes 3022848 | tf_op jit(solution)/shard_map/dot_general | solution.py:24
  44.0 1.1 convolution_convert_fusion
  45.1 1.8 %fusion.5 = bf16[1,576,1024]{2,1,0:T(8,128)(2,1)S(1)} fusion(bf16[576,1024]{1,0:T(8,128)(2,1)S(1)} %add_convert_fusion, bf16[576,576]{1,0:T(8,128)(2,1)S(1)} %convolution_convert_fusion), kind=kOutput, calls=%fused_computation.17 | convolution fusion | flops 1066291200 | bytes 3022848 | tf_op jit(solution)/shard_map/dot_general | solution.py:24
  46.9 0.7 fusion.17
  47.5 0.7 fusion.16
  48.2 0.7 fusion.15
  48.9 0.7 fusion.14
  49.6 0.7 fusion.13
  50.2 0.7 fusion.12
  50.9 0.7 fusion.11
  51.6 0.7 fusion.10
  52.3 3.6 %all-to-all-start.1 = ((bf16[8,1,72,1024]{3,2,1,0:T(8,128)(2,1)}), bf16[8,1,72,1024]{3,2,1,0:T(8,128)(2,1)S(1)}, u32[]{:S(2)}, u32[]{:S(2)}) async-start(bf16[8,1,72,1024]{3,2,1,0:T(8,128)(2,1)} %fusion.10), calls=%async_computation.1 | async-start | bytes 2359296 | tf_op jit(solution)/shard_map/all_to_all | solution.py:48
  55.8 0.0 all-gather.2.cloned.1.call-start
  55.9 1.0 sort.17
  56.9 15.6 %all-to-all-done.1 = bf16[8,1,72,1024]{3,2,1,0:T(8,128)(2,1)S(1)} async-done(((bf16[8,1,72,1024]{3,2,1,0:T(8,128)(2,1)}), bf16[8,1,72,1024]{3,2,1,0:T(8,128)(2,1)S(1)}, u32[]{:S(2)}, u32[]{:S(2)}) %all-to-all-start.1) | async-done | bytes 1179680 | tf_op jit(solution)/shard_map/all_to_all | solution.py:48
  72.5 0.6 gather_fusion.1
  73.1 0.9 broadcast_select_fusion
  74.1 0.0 all-gather.2.cloned.1.call-update
  74.1 49.5 %all-gather.2.cloned.1.call-done = bf16[16,72,1024]{2,1,0:T(8,128)(2,1)} async-done(((bf16[4,72,1024]{2,1,0:T(8,128)(2,1)}), bf16[16,72,1024]{2,1,0:T(8,128)(2,1)}) %all-gather.2.cloned.1.call-update) | async-done | bytes 2359312 | tf_op jit(solution)/shard_map/all_gather | solution.py:55
  123.6 3.3 %copy.13 = bf16[16,72,1024]{2,1,0:T(8,128)(2,1)} copy(bf16[16,72,1024]{2,1,0:T(8,128)(2,1)} %all-gather.2.cloned.1.call-done) | data formatting | bytes 4718592
  (5 shorter events, 0.0 us)
Async XLA Ops:
  32.5 1.3 copy-start
  37.7 2.0 %copy-start.1 = (bf16[1,576,1024]{2,1,0:T(8,128)(2,1)S(1)}, bf16[1,576,1024]{2,1,0:T(8,128)(2,1)}, u32[]{:S(2)}) copy-start(bf16[1,576,1024]{2,1,0:T(8,128)(2,1)} %param.4) | copy-start | bytes 3538948
  52.3 20.3 %all-to-all-start.1 = ((bf16[8,1,72,1024]{3,2,1,0:T(8,128)(2,1)}), bf16[8,1,72,1024]{3,2,1,0:T(8,128)(2,1)S(1)}, u32[]{:S(2)}, u32[]{:S(2)}) async-start(bf16[8,1,72,1024]{3,2,1,0:T(8,128)(2,1)} %fusion.10), calls=%async_computation.1 | async-start | bytes 2359296 | tf_op jit(solution)/shard_map/all_to_all | solution.py:48
  55.8 67.8 %all-gather.2.cloned.1.call-start = ((), (), s32[]{:S(2)}) async-start(), calls=%async_computation.2 | async-start | bytes 2949120 | tf_op jit(solution)/shard_map/all_gather | solution.py:55
Sparse Core Ops, SparseCore 0:
  74.2 49.3 all-gather.1
